TPU v7x, 32 devices: a whole 2x2x4 slice. The times are simulated.
32 devices in a mesh: dp: 4 (over x, core), mp: 8 (over z, y).
Axes of the slice: x: 2, y: 2, z: 4, core: 2. Of those that a mesh axis runs over, the one named last changes fastest.
Arguments:
- tokens: bfloat16 [1280, 1792], P(('dp', 'mp')), may hold values from -6 to 6
- norm_gain: float32 [1792], replicated, may hold values from 0.5 to 1.5
- norm_bias: float32 [1792], replicated, may hold values from -3 to 3
- w_in: bfloat16 [1792, 15360], P('dp', 'mp'), may hold values from -0.125 to 0.125
- b_in: float32 [15360], P('mp'), may hold values from -3 to 3
- w_out: bfloat16 [15360, 1792], P('mp', 'dp'), may hold values from -0.046875 to 0.046875
- b_out: float32 [1792], replicated, may hold values from -3 to 3
Outputs:
- result: bfloat16 [1280, 1792], P(('dp', 'mp'))
All inputs are finite; a program needn't handle non-finite values.
Results may differ from a plain program's by a relative error of at most 0.0042.
Values may be sent and summed in bfloat16 or wider, within the bound.
A program may use at most 128 MiB of HBM per device.

v0:
```python
import jax
import jax.numpy as jnp
from jax import lax
from jax.sharding import PartitionSpec as P


def on_device(tokens, norm_gain, norm_bias, w_in, b_in, w_out, b_out):
    values = tokens.astype(jnp.float32)
    center = jnp.mean(values, axis=1, keepdims=True)
    spread = jnp.mean((values - center) ** 2, axis=1, keepdims=True)
    normed = ((values - center) / jnp.sqrt(spread + 1e-06) * norm_gain + norm_bias).astype(
        jnp.bfloat16
    )
    w_in_full = lax.all_gather(w_in, "dp", axis=0, tiled=True)
    gathered = lax.all_gather(normed, "mp", axis=0, tiled=True)
    pre = jnp.dot(gathered, w_in_full, preferred_element_type=jnp.float32) + b_in
    hidden = jax.nn.gelu(pre, approximate=False).astype(jnp.bfloat16)
    w_out_full = lax.all_gather(w_out, "dp", axis=1, tiled=True)
    summed = lax.psum_scatter(
        jnp.dot(hidden, w_out_full, preferred_element_type=jnp.float32),
        "mp",
        scatter_dimension=0,
        tiled=True,
    )
    return (values + summed + b_out).astype(jnp.bfloat16)


def solution(mesh):
    placed = (P(("dp", "mp"), None), P(), P(), P("dp", "mp"), P("mp"), P("mp", "dp"), P())
    return jax.shard_map(
        on_device, mesh=mesh, in_specs=placed, out_specs=P(("dp", "mp"), None), check_vma=False
    )
```

profile of v0, /device:TPU:0, one launch (start us, length us, event | category | flops | bytes accessed | tf_op | source)
XLA Modules:
  0.0 249.3 jit_solution(16586171305829466705)
XLA Ops:
  6.5 0.0 copy-start.2
  6.5 0.0 all-gather.4.cloned.1.call-start
  6.5 1.0 convert_reduce_fusion
  7.6 1.1 fusion.45
  8.7 1.7 fusion.48
  10.5 0.0 all-gather.4.cloned.1.call-update
  10.5 0.0 all-gather.6.cloned.1.call-start
  10.5 0.7 all-gather.6.cloned.1.call-update
  11.2 0.0 all-gather.8.cloned.1.call-start
  11.3 0.7 all-gather.8.cloned.1.call-update
  12.0 0.0 copy-start
  12.0 0.0 copy-start.1
  12.0 0.0 reduce-scatter.2.cloned.1.call-start
  12.0 42.5 %all-gather.4.cloned.1.call-done = bf16[320,1792]{1,0:T(8,128)(2,1)} async-done(((bf16[40,1792]{1,0:T(8,128)(2,1)}), bf16[320,1792]{1,0:T(8,128)(2,1)}) %all-gather.4.cloned.1.call-update) | async-done | bytes 1146896 | tf_op jit(solution)/shard_map/all_gather | solution.py:15
  54.6 49.7 %all-gather.6.cloned.1.call-done = bf16[1792,1920]{1,0:T(8,128)(2,1)} async-done(((bf16[448,1920]{1,0:T(8,128)(2,1)}), bf16[1792,1920]{1,0:T(8,128)(2,1)}) %all-gather.6.cloned.1.call-update) | async-done | bytes 6881296 | tf_op jit(solution)/shard_map/all_gather | solution.py:14
  104.3 51.3 %all-gather.8.cloned.1.call-done = bf16[1920,1792]{0,1:T(8,128)(2,1)} async-done(((bf16[1920,448]{0,1:T(8,128)(2,1)}), bf16[1920,1792]{0,1:T(8,128)(2,1)}) %all-gather.8.cloned.1.call-update) | async-done | bytes 6881296 | tf_op jit(solution)/shard_map/all_gather | solution.py:18
  155.6 0.0 copy-done.2
  155.6 15.7 %fusion.10 = f32[320,1792]{1,0:T(8,128)} fusion(bf16[1920,1792]{0,1:T(8,128)(2,1)} %all-gather.8.cloned.1.call-done, bf16[320,1792]{1,0:T(8,128)(2,1)} %all-gather.4.cloned.1.call-done, bf16[1792,1920]{1,0:T(8,128)(2,1)} %all-gather.6.cloned.1.call-done, f32[1920]{0:T(1024)S(1)} %copy-done.2), kind=kOutput, calls=%fused_computation.20 | convolution fusion | flops 4444569600 | bytes 17210880 | tf_op jit(solution)/shard_map/dot_general | solution.py:20
  171.3 0.0 reduce-scatter.2.cloned.1.call-update
  171.4 69.7 %reduce-scatter.2.cloned.1.call-done = f32[40,1792]{1,0:T(8,128)} async-done(((f32[320,1792]{1,0:T(8,128)}), f32[40,1792]{1,0:T(8,128)}) %reduce-scatter.2.cloned.1.call-update) | async-done | bytes 286736 | tf_op jit(solution)/shard_map/reduce_scatter | solution.py:19
  241.1 0.0 copy-done
  241.1 0.0 copy-done.1
  241.1 1.7 fusion.50
  (2 shorter events, 0.0 us)
Async XLA Ops:
  6.5 149.1 %copy-start.2 = (f32[1920]{0:T(1024)S(1)}, f32[1920]{0:T(1024)}, u32[]{:S(2)}) copy-start(f32[1920]{0:T(1024)} %param.11) | copy-start | bytes 23044
  6.5 48.0 %all-gather.4.cloned.1.call-start = ((), (), s32[]{:S(2)}) async-start(), calls=%async_computation.1 | async-start | bytes 1290240 | tf_op jit(solution)/shard_map/all_gather | solution.py:15
  10.5 93.8 %all-gather.6.cloned.1.call-start = ((), (), s32[]{:S(2)}) async-start(), calls=%async_computation.2 | async-start | bytes 8601600 | tf_op jit(solution)/shard_map/all_gather | solution.py:14
  11.2 144.4 %all-gather.8.cloned.1.call-start = ((), (), s32[]{:S(2)}) async-start(), calls=%async_computation.3 | async-start | bytes 8601600 | tf_op jit(solution)/shard_map/all_gather | solution.py:18
  12.0 229.1 %copy-start = (bf16[40,1792]{1,0:T(8,128)(2,1)S(1)}, bf16[40,1792]{1,0:T(8,128)(2,1)}, u32[]{:S(2)}) copy-start(bf16[40,1792]{1,0:T(8,128)(2,1)} %param.7) | copy-start | bytes 430084
  12.0 229.1 %copy-start.1 = (f32[1792]{0:T(1024)S(1)}, f32[1792]{0:T(1024)}, u32[]{:S(2)}) copy-start(f32[1792]{0:T(1024)} %param.13) | copy-start | bytes 21508
  12.0 229.1 %reduce-scatter.2.cloned.1.call-start = ((), (), s32[]{:S(2)}) async-start(), calls=%async_computation.4 | async-start | bytes 2580480 | tf_op jit(solution)/shard_map/reduce_scatter | solution.py:19
Sparse Core Ops, SparseCore 0:
  10.6 43.9 all-gather.3
  56.1 48.1 all-gather.5
  105.9 49.6 all-gather.7
  171.5 69.5 reduce-scatter.1
where the time goes:
time: 249 us
  waiting for transfers between devices  215 us (86%)
  matrix products  15.7 us (6%)
  between operations  13.2 us (5%)
  other arithmetic  5.56 us (2%)
    reduce_scatter x1, waiting for transfers between devices, on_device(): lax.psum_scatter(jnp.dot(hidden, w_out_full, preferred_element_type=jnp.f...  69.7 us
    all_gather x1, waiting for transfers between devices, on_device(): w_out_full = lax.all_gather(w_out, 'dp', axis=1, tiled=True)  51.3 us
    all_gather x1, waiting for transfers between devices, on_device(): w_in_full = lax.all_gather(w_in, 'dp', axis=0, tiled=True)  49.7 us
    all_gather x1, waiting for transfers between devices, on_device(): gathered = lax.all_gather(normed, 'mp', axis=0, tiled=True)  42.5 us
    dot_general x1, matrix products, on_device(): jnp.dot(hidden, w_out_full, preferred_element_type=jnp.float32)  15.7 us
  transfers between devices with their start and end apart: 4, of which 4 were waited for; matrix products, arithmetic and copies ran while one was open for 0% of the time, Pallas kernels for 0%

commit v1 on v0

--- a/solution.py
+++ b/solution.py
@@ -15,7 +15,12 @@
     gathered = lax.all_gather(normed, "mp", axis=0, tiled=True)
     pre = jnp.dot(gathered, w_in_full, preferred_element_type=jnp.float32) + b_in
     hidden = jax.nn.gelu(pre, approximate=False).astype(jnp.bfloat16)
-    w_out_full = lax.all_gather(w_out, "dp", axis=1, tiled=True)
+    ring = [w_out]
+    for hop in range(3):
+        ring.append(lax.ppermute(ring[-1], "dp", [(dev, (dev + 1) % 4) for dev in range(4)]))
+    w_out_full = jnp.roll(
+        jnp.concatenate(ring[::-1], axis=1), (lax.axis_index("dp") + 1) * ring[0].shape[1], axis=1
+    )
     summed = lax.psum_scatter(
         jnp.dot(hidden, w_out_full, preferred_element_type=jnp.float32),
         "mp",

time: 249 us -> 216 us (0.87)
  waiting for transfers between devices: 215 us -> 164 us
  local copies, waits for them, and re-layouts: 0.02 us -> 16.7 us
    ppermute x0 -> x3, waiting for transfers between devices: none -> 86.9 us  [on_device(): lax.ppermute(ring[-1], 'dp', [(dev, (dev + 1) % 4) for dev in range(4)])]
    all_gather x1 -> x0, waiting for transfers between devices: 51.3 us -> none  [on_device(): w_out_full = lax.all_gather(w_out, 'dp', axis=1, tiled=True)]
    all_gather x1, waiting for transfers between devices: 49.7 us -> 0.01 us  [on_device(): w_in_full = lax.all_gather(w_in, 'dp', axis=0, tiled=True)]
    all_gather x1, waiting for transfers between devices: 42.5 us -> 0.01 us  [on_device(): gathered = lax.all_gather(normed, 'mp', axis=0, tiled=True)]
    unnamed x6 -> x15, local copies, waits for them, and re-layouts: 0.02 us -> 15.3 us
    reduce_scatter x1, waiting for transfers between devices: 69.7 us -> 75.9 us  [on_device(): lax.psum_scatter(jnp.dot(hidden, w_out_full, preferred_element_type=jnp.f...]
  transfers between devices with their start and end apart: 4 -> 6, of which waited for: 4 -> 4; matrix products, arithmetic and copies ran while one was open for 0% -> 8% of each run, Pallas kernels for 0% -> 0%
where the time goes in v1:
time: 216 us
  waiting for transfers between devices  164 us (76%)
  local copies, waits for them, and re-layouts  16.7 us (8%)
  matrix products  16 us (7%)
  between operations  13.1 us (6%)
  other arithmetic  5.68 us (3%)
    ppermute x3, waiting for transfers between devices, on_device(): lax.ppermute(ring[-1], 'dp', [(dev, (dev + 1) % 4) for dev in range(4)])  86.9 us
    reduce_scatter x1, waiting for transfers between devices, on_device(): lax.psum_scatter(jnp.dot(hidden, w_out_full, preferred_element_type=jnp.f...  75.9 us
    dot_general x1, matrix products, on_device(): jnp.dot(hidden, w_out_full, preferred_element_type=jnp.float32)  16 us
    unnamed x15, local copies, waits for them, and re-layouts  15.3 us
  transfers between devices with their start and end apart: 6, of which 4 were waited for; matrix products, arithmetic and copies ran while one was open for 8% of the time, Pallas kernels for 0%

profile of v1, /device:TPU:0, one launch (start us, length us, event | category | flops | bytes accessed | tf_op | source)
XLA Modules:
  0.0 215.7 jit_solution(12784724411709924408)
XLA Ops:
  6.5 0.0 copy-start
  6.5 0.0 all-gather.3.cloned.1.call-start
  6.5 1.2 convert_reduce_fusion
  7.7 1.1 fusion.46
  8.8 1.7 fusion.49
  10.6 0.0 all-gather.3.cloned.1.call-update
  10.6 0.0 all-gather.5.cloned.1.call-start
  10.6 0.7 all-gather.5.cloned.1.call-update
  11.3 0.0 reduce-scatter.2.cloned.1.call-start
  11.4 0.0 copy-done
  11.4 0.5 collective-permute-start
  11.9 21.6 %collective-permute-done = bf16[1920,448]{0,1:T(8,128)(2,1)S(1)} collective-permute-done((bf16[1920,448]{0,1:T(8,128)(2,1)S(1)}, bf16[1920,448]{0,1:T(8,128)(2,1)S(1)}, u32[]{:S(2)}, u32[]{:S(2)}) %collective-permute-start) | collective-permute-done | bytes 1720352 | tf_op jit(solution)/shard_map/ppermute | solution.py:20
  33.5 0.0 collective-permute-start.1
  33.5 21.5 %collective-permute-done.1 = bf16[1920,448]{0,1:T(8,128)(2,1)} collective-permute-done((bf16[1920,448]{0,1:T(8,128)(2,1)S(1)}, bf16[1920,448]{0,1:T(8,128)(2,1)}, u32[]{:S(2)}, u32[]{:S(2)}) %collective-permute-start.1) | collective-permute-done | bytes 1720352 | tf_op jit(solution)/shard_map/ppermute | solution.py:20
  55.1 0.0 collective-permute-start.2
  55.1 43.8 %collective-permute-done.2 = bf16[1920,448]{0,1:T(8,128)(2,1)} collective-permute-done((bf16[1920,448]{0,1:T(8,128)(2,1)}, bf16[1920,448]{0,1:T(8,128)(2,1)}, u32[]{:S(2)}, u32[]{:S(2)}) %collective-permute-start.2) | collective-permute-done | bytes 1720352 | tf_op jit(solution)/shard_map/ppermute | solution.py:20
  98.9 2.8 %constant_dynamic-update-slice_fusion.7 = bf16[1920,3584]{0,1:T(8,128)(2,1)} fusion(bf16[1920,448]{0,1:T(8,128)(2,1)} %collective-permute-done.2), kind=kLoop, calls=%fused_computation.71 | loop fusion | bytes 3440640
  101.7 2.8 %constant_dynamic-update-slice_fusion.6 = bf16[1920,3584]{0,1:T(8,128)(2,1)} fusion(bf16[1920,3584]{0,1:T(8,128)(2,1)} %constant_dynamic-update-slice_fusion.7, bf16[1920,448]{0,1:T(8,128)(2,1)} %collective-permute-done.1), kind=kLoop, calls=%fused_computation.70 | loop fusion | bytes 3440640
  104.4 1.3 constant_dynamic-update-slice_fusion.5
  105.8 1.4 constant_dynamic-update-slice_fusion.4
  107.2 2.8 %constant_dynamic-update-slice_fusion.3 = bf16[1920,3584]{0,1:T(8,128)(2,1)} fusion(bf16[1920,3584]{0,1:T(8,128)(2,1)} %constant_dynamic-update-slice_fusion.4, bf16[1920,448]{0,1:T(8,128)(2,1)} %collective-permute-done.2), kind=kLoop, calls=%fused_computation.67 | loop fusion | bytes 3440640
  110.0 2.8 %constant_dynamic-update-slice_fusion.2 = bf16[1920,3584]{0,1:T(8,128)(2,1)} fusion(bf16[1920,3584]{0,1:T(8,128)(2,1)} %constant_dynamic-update-slice_fusion.3, bf16[1920,448]{0,1:T(8,128)(2,1)} %collective-permute-done.1), kind=kLoop, calls=%fused_computation.66 | loop fusion | bytes 3440640
  112.8 1.3 constant_dynamic-update-slice_fusion.1
  114.2 0.0 copy-start.3
  114.2 1.4 constant_dynamic-update-slice_fusion
  115.6 0.0 copy-start.1
  115.6 0.0 copy-start.2
  115.6 0.0 all-gather.3.cloned.1.call-done
  115.6 0.0 all-gather.5.cloned.1.call-done
  115.6 0.0 copy-done.3
  115.6 16.0 %fusion = f32[320,1792]{1,0:T(8,128)} fusion(bf16[1920,3584]{0,1:T(8,128)(2,1)} %constant_dynamic-update-slice_fusion, s32[]{:T(128)S(6)} %select_n.14, bf16[320,1792]{1,0:T(8,128)(2,1)} %all-gather.3.cloned.1.call-done, bf16[1792,1920]{1,0:T(8,128)(2,1)} %all-gather.5.cloned.1.call-done, f32[1920]{0:T(1024)S(1)} %copy-done.3), kind=kOutput, calls=%fused_computation | convolution fusion | flops 4444569600 | bytes 17210884 | tf_op jit(solution)/shard_map/dot_general | solution.py:25
  131.6 0.0 reduce-scatter.2.cloned.1.call-update
  131.7 75.9 %reduce-scatter.2.cloned.1.call-done = f32[40,1792]{1,0:T(8,128)} async-done(((f32[320,1792]{1,0:T(8,128)}), f32[40,1792]{1,0:T(8,128)}) %reduce-scatter.2.cloned.1.call-update) | async-done | bytes 286736 | tf_op jit(solution)/shard_map/reduce_scatter | solution.py:24
  207.5 0.0 copy-done.1
  207.5 0.0 copy-done.2
  207.5 1.7 fusion.51
  (2 shorter events, 0.0 us)
Async XLA Ops:
  6.5 4.9 %copy-start = (bf16[1920,448]{0,1:T(8,128)(2,1)S(1)}, bf16[1920,448]{0,1:T(8,128)(2,1)}, u32[]{:S(2)}) copy-start(bf16[1920,448]{0,1:T(8,128)(2,1)} %param.12) | copy-start | bytes 5160964
  6.5 109.0 %all-gather.3.cloned.1.call-start = ((), (), s32[]{:S(2)}) async-start(), calls=%async_computation.1 | async-start | bytes 1290240 | tf_op jit(solution)/shard_map/all_gather | solution.py:15
  10.6 105.0 %all-gather.5.cloned.1.call-start = ((), (), s32[]{:S(2)}) async-start(), calls=%async_computation.2 | async-start | bytes 8601600 | tf_op jit(solution)/shard_map/all_gather | solution.py:14
  11.3 196.2 %reduce-scatter.2.cloned.1.call-start = ((), (), s32[]{:S(2)}) async-start(), calls=%async_computation.3 | async-start | bytes 2580480 | tf_op jit(solution)/shard_map/reduce_scatter | solution.py:24
  11.4 22.1 %collective-permute-start = (bf16[1920,448]{0,1:T(8,128)(2,1)S(1)}, bf16[1920,448]{0,1:T(8,128)(2,1)S(1)}, u32[]{:S(2)}, u32[]{:S(2)}) collective-permute-start(bf16[1920,448]{0,1:T(8,128)(2,1)S(1)} %copy-done), channel_id=1, source_target_pairs={{0,8},{8,16},{16,24},{24,0},{1,9},{9,17},{17,25},{25,1},{2,10},{10... | collective-permute-start | bytes 5160968 | tf_op jit(solution)/shard_map/ppermute | solution.py:20
  33.5 21.5 %collective-permute-start.1 = (bf16[1920,448]{0,1:T(8,128)(2,1)S(1)}, bf16[1920,448]{0,1:T(8,128)(2,1)}, u32[]{:S(2)}, u32[]{:S(2)}) collective-permute-start(bf16[1920,448]{0,1:T(8,128)(2,1)S(1)} %collective-permute-done), channel_id=1, source_target_pairs={{0,8},{8,16},{16,24},{24,0},{1,9},{9,17},{17,25},{25,1},{2,10},{10... | collective-permute-start | bytes 5160968 | tf_op jit(solution)/shard_map/ppermute | solution.py:20
  55.1 43.8 %collective-permute-start.2 = (bf16[1920,448]{0,1:T(8,128)(2,1)}, bf16[1920,448]{0,1:T(8,128)(2,1)}, u32[]{:S(2)}, u32[]{:S(2)}) collective-permute-start(bf16[1920,448]{0,1:T(8,128)(2,1)} %collective-permute-done.1), channel_id=1, source_target_pairs={{0,8},{8,16},{16,24},{24,0},{1,9},{9,17},{17,25},{25,1},{2,10},{10... | collective-permute-start | bytes 5160968 | tf_op jit(solution)/shard_map/ppermute | solution.py:20
  114.2 1.4 copy-start.3
  115.6 92.0 %copy-start.1 = (bf16[40,1792]{1,0:T(8,128)(2,1)S(1)}, bf16[40,1792]{1,0:T(8,128)(2,1)}, u32[]{:S(2)}) copy-start(bf16[40,1792]{1,0:T(8,128)(2,1)} %param.7) | copy-start | bytes 430084
  115.6 92.0 %copy-start.2 = (f32[1792]{0:T(1024)S(1)}, f32[1792]{0:T(1024)}, u32[]{:S(2)}) copy-start(f32[1792]{0:T(1024)} %param.13) | copy-start | bytes 21508
Sparse Core Ops, SparseCore 0:
  10.7 43.6 all-gather.2
  56.0 59.2 all-gather.4
  131.8 75.7 reduce-scatter.1
